TPU v7x, 128 devices: a whole 4x4x4 slice. The times are simulated.
128 devices in a mesh: row: 8 (over z_hi, x), col: 16 (over z_lo, y, core).
Axes of the slice: x: 4, y: 4, z: 4 (z_hi: 2, z_lo: 2; z = z_hi * 2 + z_lo), core: 2. Of those that a mesh axis runs over, the one named last changes fastest.
Arguments:
- tokens: bfloat16 [16384, 2048], P(('row', 'col')), may hold values from -6 to 6
- expert_ids: int32 [16384, 8], P(('row', 'col')), may hold values from 0 to 127, all different within a row; in each aligned block of 128 rows (0 to 127, 128 to 255, ...) at most 10 rows name the same one
- gate_probs: float32 [16384, 8], P(('row', 'col')), may hold values from 0.05 to 0.5
- w_gate: bfloat16 [128, 2048, 768], P(('row', 'col')), may hold values from -0.125 to 0.125
- w_up: bfloat16 [128, 2048, 768], P(('row', 'col')), may hold values from -0.125 to 0.125
- w_down: bfloat16 [128, 768, 2048], P(('row', 'col')), may hold values from -0.21875 to 0.21875
Outputs:
- mixed: bfloat16 [16384, 2048], P(('row', 'col'))
Inputs may be any that keep to these rules, and one draw needn't show every extreme that they name: `expert_ids`: each row names 8 different experts; among the rows of one device (aligned blocks of 128 rows) no expert is named more than 10 times.
All inputs are finite; a program needn't handle non-finite values.
Results may differ from a plain program's by a relative error of at most 0.0058.
Values may be sent and summed in bfloat16 or wider, within the bound.
A program may use at most 128 MiB of HBM per device.

v0:
```python
import functools
import math

import jax
import jax.numpy as jnp
from jax import lax
from jax.experimental import pallas as pl
from jax.experimental.pallas import tpu as pltpu
from jax.sharding import PartitionSpec as P

MESH = pl.DeviceIdType.MESH
BF16 = jnp.bfloat16
F32 = jnp.float32
PIECES = 2


def moe_kernel(
    rows, cols, slots, group, pieces,
    ids_in, probs_in, tok_in, wg_in, wu_in, wd_in, out_ref,
    ids_all, probs_all, tok, wg, wu, wd, disp, comb, hid, xs, xr, yr, pr, acc, zs, zr,
    load_sem, ids_send, ids_recv, probs_send, probs_recv, ztok_send, ztok_recv, ctok_send, ctok_recv,
    x_send, x_recv, y_send, y_recv, p_send, p_recv, z_send, z_recv,
):
    r = lax.axis_index("row")
    c = lax.axis_index("col")
    chips = cols // 2
    chip, core = c // 2, c % 2
    mate = 2 * chip + (1 - core)
    count, width = tok_in.shape
    per = group // 2
    chunks = chips // per
    part = group * slots
    total = rows * part
    hidden = wg.shape[1]
    f_tile = math.gcd(hidden, 256)
    d_tile = math.gcd(width // pieces, 512)
    piece = width // pieces

    def remote(src, dst, send, recv, row, col):
        return pltpu.make_async_remote_copy(
            src_ref=src, dst_ref=dst, send_sem=send, recv_sem=recv,
            device_id=(row, col), device_id_type=MESH,
        )

    short = jnp.minimum(chip, chips - 1 - chip)
    side = jnp.where(2 * chip < chips, 1, -1)
    order, signs = [chip], [None]
    for p in range(1, chips):
        both = p <= 2 * short
        sign = jnp.where(both, 1 if p % 2 else -1, side)
        far = jnp.where(both, (p + 1) // 2, p - short)
        order.append(chip + sign * far)
        signs.append(sign)

    load_tok = pltpu.make_async_copy(tok_in, tok.at[chip, 0], load_sem.at[0])
    load_ids = pltpu.make_async_copy(ids_in, ids_all.at[chip, 0], load_sem.at[1])
    load_probs = pltpu.make_async_copy(probs_in, probs_all.at[chip, 0], load_sem.at[5])
    load_w = [
        pltpu.make_async_copy(wg_in.at[0], wg, load_sem.at[2]),
        pltpu.make_async_copy(wu_in.at[0], wu, load_sem.at[3]),
        pltpu.make_async_copy(wd_in.at[0], wd, load_sem.at[4]),
    ]
    load_tok.start()
    load_ids.start()
    load_probs.start()

    barrier = pltpu.get_barrier_semaphore()
    for d in range(1, cols):
        pl.semaphore_signal(barrier, inc=1, device_id=(r, (c + d) % cols), device_id_type=MESH)
    for j in range(1, rows):
        pl.semaphore_signal(barrier, inc=1, device_id=((r + j) % rows, c), device_id_type=MESH)
    pl.semaphore_wait(barrier, cols - 1 + rows - 1)

    def hop(q, send, to):
        return remote(
            tok.at[q, 0], tok.at[q, 0], ztok_send.at[send], ztok_recv.at[q],
            r, 2 * ((to + chips) % chips) + core,
        )

    def onward(p, act):
        if p == 0:
            @pl.when(chip > 0)
            def _():
                act(hop(chip, 0, chip - 1))

            @pl.when(chip < chips - 1)
            def _():
                act(hop(chip, chips, chip + 1))
        else:
            to = chip - signs[p]

            @pl.when((to >= 0) & (to < chips))
            def _():
                act(hop(order[p], p, to))

    ctok = [
        remote(tok.at[q, 0], tok.at[q, 1], ctok_send.at[p], ctok_recv.at[p], r, mate)
        for p, q in enumerate(order)
    ]
    load_tok.wait()
    ctok[0].start()
    load_ids.wait()
    load_probs.wait()

    def routing(d, t, slot):
        far, other = d // 2, d % 2
        to = 2 * t + (core if other == 0 else 1 - core)
        return (
            remote(
                ids_all.at[chip, 0], ids_all.at[slot, other],
                ids_send.at[d], ids_recv.at[slot, other], r, to,
            ),
            remote(
                probs_all.at[chip, 0], probs_all.at[slot, other],
                probs_send.at[d], probs_recv.at[slot, other], r, to,
            ),
        )

    for d in range(1, cols):
        for copy in routing(d, (chip + d // 2) % chips, chip):
            copy.start()
    onward(0, lambda copy: copy.start())
    for copy in load_w:
        copy.start()
    for d in range(1, cols):
        t = (chip + d // 2) % chips
        for copy in routing(d, t, t):
            copy.wait()

    earlier = (
        lax.broadcasted_iota(jnp.int32, (count, count), 0)
        < lax.broadcasted_iota(jnp.int32, (count, count), 1)
    ).astype(BF16)
    slot_of = lax.broadcasted_iota(jnp.int32, (part, count), 0).astype(F32)
    lane_rows = 16
    row_id = lax.broadcasted_iota(jnp.int32, (lane_rows, count), 0)

    def route(i):
        for s in range(group):
            ids = ids_all[order[i * per + s // 2], s % 2]
            probs = probs_all[order[i * per + s // 2], s % 2]
            named = jnp.zeros((lane_rows, count), F32)
            weights = []
            for j in range(rows):
                expert = ((r + j) % rows) * cols + c
                hit = (ids == expert).astype(F32)
                named = jnp.where(row_id == j, jnp.sum(hit, axis=0, keepdims=True), named)
                weights.append(jnp.sum(hit * probs, axis=0, keepdims=True))
            rank = jnp.dot(named.astype(BF16), earlier, preferred_element_type=F32)
            key = jnp.where(named > 0.5, rank + float(s * slots), -1.0)
            for j in range(rows):
                one = (slot_of == key[j:j + 1, :]).astype(F32)
                disp[j * part:(j + 1) * part, s * count:(s + 1) * count] = one.astype(BF16)
                comb[i, j * part:(j + 1) * part, s * count:(s + 1) * count] = (
                    one * weights[j]
                ).astype(BF16)

    x_out, y_out, p_out, z_out = {}, {}, {}, {}

    def dispatch(i):
        for d in range(i * per, (i + 1) * per):
            if d > 0:
                hop(order[d], d, chip).wait_recv()
                onward(d, lambda copy: copy.start())
                ctok[d].start()
        route(i)
        for d in range(i * per, (i + 1) * per):
            ctok[d].wait_recv()

        def tile(n, _):
            at = pl.ds(pl.multiple_of(n * d_tile, d_tile), d_tile)
            block = jnp.concatenate(
                [tok[q, :, :, at].reshape(2 * count, d_tile) for q in order[i * per:(i + 1) * per]]
            )
            res = jnp.dot(disp[...], block, preferred_element_type=F32).astype(BF16)
            xr[i, 0, :, at] = res[:part]
            xs[i, :, :, at] = res[part:].reshape(rows - 1, part, d_tile)
            return 0

        lax.fori_loop(0, width // d_tile, tile, 0)
        for j in range(1, rows):
            copy = remote(
                xs.at[i, j - 1], xr.at[i, j], x_send.at[i, j], x_recv.at[i, j],
                (r + j) % rows, c,
            )
            copy.start()
            x_out[i, j] = copy

    def experts(i, first):
        for j in range(1, rows):
            x_out[i, j].wait()
        if first:
            for copy in load_w:
                copy.wait()

        def up_tile(n, _):
            at = pl.ds(pl.multiple_of(n * f_tile, f_tile), f_tile)
            x = xr[i].reshape(total, width)
            gate = jnp.dot(x, wg[:, at], preferred_element_type=F32)
            up = jnp.dot(x, wu[:, at], preferred_element_type=F32)
            hid[:, at] = (gate / (1.0 + jnp.exp(-gate)) * up).astype(BF16)
            return 0

        lax.fori_loop(0, hidden // f_tile, up_tile, 0)

        def down_tile(n, _):
            at = pl.ds(pl.multiple_of(n * d_tile, d_tile), d_tile)
            res = jnp.dot(hid[...], wd[:, at], preferred_element_type=F32).astype(BF16)
            yr[i, 0, :, at] = res[:part]
            xs[i, :, :, at] = res[part:].reshape(rows - 1, part, d_tile)
            return 0

        for h in range(pieces):
            at = pl.ds(h * piece, piece)
            lax.fori_loop(h * piece // d_tile, (h + 1) * piece // d_tile, down_tile, 0)
            for j in range(1, rows):
                copy = remote(
                    xs.at[i, j - 1, :, at], yr.at[i, j, :, at],
                    y_send.at[i, j, h], y_recv.at[i, j, h], (r + rows - j) % rows, c,
                )
                copy.start()
                y_out[i, j, h] = copy

    def combine(i, h):
        for j in range(1, rows):
            y_out[i, j, h].wait()

        def tile(n, _):
            at = pl.ds(pl.multiple_of(n * d_tile, d_tile), d_tile)
            y = yr[i, :, :, at].reshape(total, d_tile)
            res = lax.dot_general(
                comb[i], y, (((0,), (0,)), ((), ())), preferred_element_type=F32
            )
            for p in range(per):
                d = i * per + p
                acc[d, :, at] = res[2 * p * count:(2 * p + 1) * count]
                tok[order[d], 1, :, at] = res[(2 * p + 1) * count:(2 * p + 2) * count].astype(BF16)
            return 0

        lax.fori_loop(h * piece // d_tile, (h + 1) * piece // d_tile, tile, 0)
        at = pl.ds(h * piece, piece)
        for d in range(i * per, (i + 1) * per):
            copy = remote(
                tok.at[order[d], 1, :, at], pr.at[d, :, at], p_send.at[d, h], p_recv.at[d, h],
                r, mate,
            )
            copy.start()
            p_out[d, h] = copy

    def partial_copy(d, h, slot):
        at = pl.ds(h * piece, piece)
        return remote(
            zs.at[d - 1, :, at], zr.at[slot, :, at], z_send.at[d, h], z_recv.at[slot, h],
            r, 2 * order[d] + core,
        )

    def reduce_cores(i, h):
        at = pl.ds(h * piece, piece)
        for d in range(i * per, (i + 1) * per):
            p_out[d, h].wait()
            if d > 0:
                zs[d - 1, :, at] = (acc[d, :, at] + pr[d, :, at].astype(F32)).astype(BF16)
                partial_copy(d, h, chip).start()

    turn = list(range(chunks // 2, chunks)) + list(range(chunks // 2 - 1, -1, -1))
    for i in range(chunks):
        dispatch(i)
    for n in range(chunks):
        experts(turn[n], n == 0)
    for n in range(chunks):
        for h in range(pieces):
            combine(turn[n], h)
            reduce_cores(turn[n], h)
    for h in range(pieces):
        at = pl.ds(h * piece, piece)
        result = acc[0, :, at] + pr[0, :, at].astype(F32)
        for d in range(1, chips):
            partial_copy(d, h, order[d]).wait()
            result = result + zr[order[d], :, at].astype(F32)
        out_ref[:, at] = result.astype(BF16)
    for d in range(chips):
        onward(d, lambda copy: copy.wait_send())
        ctok[d].wait_send()


def body(tokens, expert_ids, gate_probs, w_gate, w_up, w_down):
    count, choices = expert_ids.shape
    width = tokens.shape[1]
    hidden = w_gate.shape[2]
    rows = lax.axis_size("row")
    cols = lax.axis_size("col")
    slots = 5 * count * choices // (4 * rows * cols * w_gate.shape[0])
    group = 2
    while group * slots % 16:
        group *= 2
    chips = cols // 2
    chunks = cols // group
    part = group * slots
    any_spec = pl.BlockSpec(memory_space=pl.ANY)
    dma = pltpu.SemaphoreType.DMA
    scratch = [
        pltpu.VMEM((chips, 2, choices, count), jnp.int32),
        pltpu.VMEM((chips, 2, choices, count), F32),
        pltpu.VMEM((chips, 2, count, width), BF16),
        pltpu.VMEM((width, hidden), BF16),
        pltpu.VMEM((width, hidden), BF16),
        pltpu.VMEM((hidden, width), BF16),
        pltpu.VMEM((rows * part, group * count), BF16),
        pltpu.VMEM((chunks, rows * part, group * count), BF16),
        pltpu.VMEM((rows * part, hidden), BF16),
        pltpu.VMEM((chunks, rows - 1, part, width), BF16),
        pltpu.VMEM((chunks, rows, part, width), BF16),
        pltpu.VMEM((chunks, rows, part, width), BF16),
        pltpu.VMEM((chips, count, width), BF16),
        pltpu.VMEM((chips, count, width), F32),
        pltpu.VMEM((chips - 1, count, width), BF16),
        pltpu.VMEM((chips, count, width), BF16),
        dma((6,)),
        dma((cols,)), dma((chips, 2)),
        dma((cols,)), dma((chips, 2)),
        dma((chips + 1,)), dma((chips,)),
        dma((chips,)), dma((chips,)),
        dma((chunks, rows)), dma((chunks, rows)),
        dma((chunks, rows, PIECES)), dma((chunks, rows, PIECES)),
        dma((chips, PIECES)), dma((chips, PIECES)),
        dma((chips, PIECES)), dma((chips, PIECES)),
    ]
    return pl.pallas_call(
        functools.partial(moe_kernel, rows, cols, slots, group, PIECES),
        out_shape=jax.ShapeDtypeStruct((count, width), BF16),
        in_specs=[any_spec] * 6,
        out_specs=pl.BlockSpec(memory_space=pltpu.VMEM),
        scratch_shapes=scratch,
        compiler_params=pltpu.CompilerParams(
            collective_id=0, has_side_effects=True, vmem_limit_bytes=67043328
        ),
    )(expert_ids.T, gate_probs.T, tokens, w_gate, w_up, w_down)


def solution(mesh):
    in_specs = (
        P(("row", "col"), None),
        P(("row", "col"), None),
        P(("row", "col"), None),
        P(("row", "col"), None, None),
        P(("row", "col"), None, None),
        P(("row", "col"), None, None),
    )
    out_specs = P(("row", "col"), None)
    return jax.shard_map(body, mesh=mesh, in_specs=in_specs, out_specs=out_specs, check_vma=False)
```

profile of v0, /device:TPU:46, one launch (start us, length us, event | category | flops | bytes accessed | tf_op | source)
XLA Modules:
  0.0 295.9 jit_solution(17262460616136180674)
XLA Ops:
  0.0 294.0 %shard_map.64 = bf16[128,2048]{1,0:T(8,128)(2,1)} custom-call(s32[8,128]{1,0:T(8,128)} %bitcast.2, f32[8,128]{1,0:T(8,128)} %bitcast.3, bf16[128,2048]{1,0:T(8,128)(2,1)} %tok_in.1, bf16[1,2048,768]{2,1,0:T(8,128)(2,1)} %wg_in.1, bf16[1,2048,768]{2,1,0:T(8,128)(2,1)} %wu_in.1, bf16[1,768,2048]{2,1,0:T(8,128)(2,1)} %wd_in.1), custom_call_target="tpu_custom_call" | custom-call | tf_op jit(solution)/shard_map/pallas_call | solution.py:328
  294.0 1.9 copy.8
where the time goes:
time: 296 us
  Pallas kernels  294 us (99%)
    pallas_call x1, Pallas kernels, body(): pl.pallas_call(functools.partial(moe_kernel, rows, cols, slots, group, PI...  294 us

commit v1 on v0

v1 whole, which is shorter than its diff:
```python
import functools

import jax
import jax.numpy as jnp
from jax import lax
from jax.experimental import pallas as pl
from jax.experimental.pallas import tpu as pltpu
from jax.sharding import PartitionSpec as P

MESH = pl.DeviceIdType.MESH
BF16 = jnp.bfloat16
F32 = jnp.float32
SIDE = 4
PIECES = (
    (0, 0, 384), (1, 384, 384), (2, 768, 384),
    (0, 1152, 384), (1, 1536, 256), (2, 1792, 256),
)
HALF = 1152
PLANES = ((2, 1), (2, 0), (0, 1))
ORDER = tuple((i, j) for i in range(SIDE) for j in range(SIDE) if i or j)
LINE = (1, 3, 2)
UNNAMED = -1024.0


def moe_kernel(
    slots,
    ids_in, probs_in, tok_in, wg_in, wu_in, wd_in, out_ref, *scratch,
):
    n = len(PIECES)
    tokg, scratch = scratch[:n], scratch[n:]
    xs, scratch = scratch[:n], scratch[n:]
    yr, scratch = scratch[:n], scratch[n:]
    pr, scratch = scratch[:n], scratch[n:]
    zr, scratch = scratch[:n], scratch[n:]
    (
        ids, probs, wg, wu, wd, kw_out, kw_in, kf, sel, swap, spread, xc, acc, hid, hidp,
        load_sem, k_send, k_recv, l_send, l_recv, m_send, m_recv, x_send, x_recv,
        y_send, y_recv, p_send, p_recv, z_send, z_recv,
    ) = scratch
    r = lax.axis_index("row")
    c = lax.axis_index("col")
    core = c % 2
    sign = 1 - 2 * core
    here = (r % SIDE, (c // 2) % SIDE, 2 * (r // SIDE) + c // 8)
    near = [[(h + sign * d + SIDE) % SIDE for d in range(SIDE)] for h in here]
    row_x = near[0]
    col_y = [2 * v for v in near[1]]
    row_z = [SIDE * (v // 2) for v in near[2]]
    col_z = [8 * (v % 2) for v in near[2]]
    tokens = tok_in.shape[0]
    hidden = wg.shape[1]
    group = 2 * SIDE * slots
    slab = SIDE * group
    total = SIDE * slab

    def device(d, to_core):
        return (row_z[d[2]] + row_x[d[0]], col_z[d[2]] + col_y[d[1]] + to_core)

    def remote(src, dst, send, recv, to):
        return pltpu.make_async_remote_copy(
            src_ref=src, dst_ref=dst, send_sem=send, recv_sem=recv,
            device_id=to, device_id_type=MESH,
        )

    def on_line(t, d):
        step = [0, 0, 0]
        step[t] = d
        return tuple(step)

    def in_plane(t, i, j):
        step = [0, 0, 0]
        step[PLANES[t][0]] = i
        step[PLANES[t][1]] = j
        return tuple(step)

    load_ids = pltpu.make_async_copy(ids_in, ids, load_sem.at[0])
    load_probs = pltpu.make_async_copy(probs_in, probs, load_sem.at[1])
    load_ids.start()
    load_probs.start()
    load_tok = []
    for p, (t, first, width) in enumerate(PIECES):
        copy = pltpu.make_async_copy(
            tok_in.at[:, pl.ds(first, width)], tokg[p].at[here[t], core], load_sem.at[5 + p]
        )
        copy.start()
        load_tok.append(copy)
    barrier = pltpu.get_barrier_semaphore()
    signals = 0
    for dx in range(SIDE):
        for dy in range(SIDE):
            for dz in range(SIDE):
                zeros = (dx == 0) + (dy == 0) + (dz == 0)
                if zeros in (1, 2):
                    pl.semaphore_signal(
                        barrier, inc=1, device_id=device((dx, dy, dz), core), device_id_type=MESH
                    )
                    signals += 1
                if zeros in (2, 3):
                    pl.semaphore_signal(
                        barrier, inc=1, device_id=device((dx, dy, dz), 1 - core),
                        device_id_type=MESH,
                    )
                    signals += 1

    load_ids.wait()
    load_probs.wait()
    load_w = [
        pltpu.make_async_copy(wg_in.at[0], wg, load_sem.at[2]),
        pltpu.make_async_copy(wu_in.at[0], wu, load_sem.at[3]),
        pltpu.make_async_copy(wd_in.at[0], wd, load_sem.at[4]),
    ]
    experts = ids.shape[0] * 16
    place = lax.broadcasted_iota(jnp.int32, (experts, tokens), 0)
    line_of = jnp.right_shift(place, 5)
    core_of = jnp.bitwise_and(jnp.right_shift(place, 4), 1)
    slow_of = jnp.bitwise_and(jnp.right_shift(place, 2), 3)
    fast_of = jnp.bitwise_and(place, 3)
    earlier = (
        lax.broadcasted_iota(jnp.int32, (tokens, tokens), 0)
        < lax.broadcasted_iota(jnp.int32, (tokens, tokens), 1)
    ).astype(BF16)
    for t in range(3):
        at = [None] * 3
        at[t], at[PLANES[t][0]], at[PLANES[t][1]] = line_of, slow_of, fast_of
        expert = (
            16 * (SIDE * jnp.right_shift(at[2], 1) + at[0])
            + 8 * jnp.bitwise_and(at[2], 1) + 2 * at[1] + core_of
        )
        named = jnp.zeros((experts, tokens), F32)
        weight = jnp.zeros((experts, tokens), F32)
        for k in range(ids.shape[0]):
            hit = ids[k:k + 1, :] == expert
            named = jnp.where(hit, 1.0, named)
            weight = jnp.where(hit, probs[k:k + 1, :], weight)
        rank = jnp.dot(named.astype(BF16), earlier, preferred_element_type=F32)
        key = jnp.where(named > 0.5, rank, UNNAMED).astype(BF16)
        weight = weight.astype(BF16)
        for l in range(SIDE):
            for o in range(2):
                rows = slice((2 * l + o) * 16, (2 * l + o + 1) * 16)
                kw_out[t, l, o, 0] = key[rows]
                kw_out[t, l, o, 1] = weight[rows]
        kw_in[t, 2 * here[t] + core] = kw_out[t, here[t], core]

    pl.semaphore_wait(barrier, signals)

    k_copies = []
    for t in range(3):
        for d in range(SIDE):
            for o in range(2):
                if d == 0 and o == 0:
                    continue
                to_core = core if o == 0 else 1 - core
                copy = remote(
                    kw_out.at[t, near[t][d], to_core], kw_in.at[t, 2 * here[t] + core],
                    k_send.at[t, d, o], k_recv.at[t, d, o], device(on_line(t, d), to_core),
                )
                copy.start()
                k_copies.append(copy)

    l_copies = {}
    m_copies = {}

    def to_mate(p, d):
        t = PIECES[p][0]
        block = tokg[p].at[near[t][(SIDE - d) % SIDE], core]
        copy = remote(
            block, block, m_send.at[p, d], m_recv.at[p, d], device((0, 0, 0), 1 - core)
        )
        copy.start()
        m_copies[p, d] = copy

    for p, (t, first, width) in enumerate(PIECES):
        load_tok[p].wait()
        for d in LINE:
            block = tokg[p].at[here[t], core]
            copy = remote(
                block, block, l_send.at[p, d], l_recv.at[p, d], device(on_line(t, d), core)
            )
            copy.start()
            l_copies[p, d] = copy
        to_mate(p, 0)
    for copy in load_w:
        copy.start()

    row_id = lax.broadcasted_iota(jnp.int32, (slab, slab), 0)
    col_id = lax.broadcasted_iota(jnp.int32, (slab, slab), 1)
    pair = 2 * slots
    twin = jnp.zeros((slab, slab), jnp.int32)
    for i in range(SIDE):
        for j in range(SIDE):
            first = (i * SIDE + j) * pair
            twin = jnp.where(
                (col_id >= first) & (col_id < first + pair),
                col_id + ((j * SIDE + i) * pair - first), twin,
            )
    swap[...] = (row_id == twin).astype(F32).astype(BF16)
    lane = lax.broadcasted_iota(jnp.int32, (16, total), 1)
    owner = group * lax.broadcasted_iota(jnp.int32, (16, total), 0)
    spread[...] = ((lane >= owner) & (lane < owner + group)).astype(F32).astype(BF16)

    for copy in k_copies:
        copy.wait()
    slot_of = lax.broadcasted_iota(jnp.int32, (group, tokens), 0).astype(F32)
    for t in range(3):
        def choose(s, _):
            kf[...] = kw_in[t, s, 0].astype(F32) + (s * slots).astype(F32)
            lanes = pl.ds(pl.multiple_of(s * tokens, tokens), tokens)
            for q in range(SIDE * SIDE):
                sel[t, q * group:(q + 1) * group, lanes] = (
                    slot_of == kf[q:q + 1, :]
                ).astype(F32).astype(BF16)
            return 0

        lax.fori_loop(0, 2 * SIDE, choose, 0)

    sources = 2 * SIDE * tokens
    x_copies = {}

    def forward(p):
        for d in LINE:
            l_copies[p, d].wait_recv()
            to_mate(p, d)

    def dispatch(p):
        t, first, width = PIECES[p]
        a, b = PLANES[t]
        for d in range(SIDE):
            m_copies[p, d].wait_recv()

        def select(i, _):
            rows = pl.ds(pl.multiple_of(i * slab, slab), slab)
            res = jnp.dot(
                sel[t, rows, :sources], tokg[p][...].reshape(sources, width),
                preferred_element_type=F32,
            )
            xs[p][i] = res.astype(BF16).reshape(SIDE, group, width)
            return 0

        lax.fori_loop(0, SIDE, select, 0)
        columns = pl.ds(first, width)
        for o, (i, j) in enumerate(ORDER):
            copy = remote(
                xs[p].at[near[a][i], near[b][j]], xc.at[here[a], here[b], :, columns],
                x_send.at[p, o], x_recv.at[p, o], device(in_plane(t, i, j), core),
            )
            copy.start()
            x_copies[p, o] = copy
        xc[here[a], here[b], :, columns] = xs[p][here[a], here[b]]

    for p in range(3):
        forward(p)
    for p in range(3):
        dispatch(p)
    for p in range(3, n):
        forward(p)
    for p in range(3, n):
        dispatch(p)

    lane = lax.broadcasted_iota(jnp.int32, (1, total), 1)
    slot_at = lane
    for q in range(1, SIDE * SIDE):
        slot_at = jnp.where(lane >= q * group, lane - q * group, slot_at)
    slot_at = slot_at.astype(F32)
    for t in range(3):
        def weigh(s, _):
            expand = lambda w: lax.dot_general(
                kw_in[t, s, w], spread[...], (((0,), (0,)), ((), ())),
                preferred_element_type=F32,
            )
            chosen = expand(0) + (s * slots).astype(F32) == slot_at
            value = jnp.where(chosen, expand(1), 0.0).astype(BF16)
            o, l = s // SIDE, s % SIDE
            return value

        def weigh_all(l, _):
            for o in range(2):
                rows = pl.ds(pl.multiple_of((o * SIDE + l) * tokens, tokens), tokens)
                sel[t, rows, :] = weigh(2 * l + o, 0)
            return 0

        lax.fori_loop(0, SIDE, weigh_all, 0)

    def collect(p):
        t, first, width = PIECES[p]
        for o in range(len(ORDER)):
            x_copies[p, o].wait()
        if t == 0:
            return
        columns = pl.ds(first, width)

        def reorder(i, _):
            block = xc.at[i] if t == 1 else xc.at[:, i]
            res = jnp.dot(
                swap[...], block[:, :, columns].reshape(slab, width), preferred_element_type=F32
            )
            block[:, :, columns] = res.astype(BF16).reshape(SIDE, group, width)
            return 0

        lax.fori_loop(0, SIDE, reorder, 0)

    m_rows = 2 * slab
    f_tile = 256

    def up_tiles(step):
        def one(k, _):
            for m in range(2):
                step(m, pl.multiple_of(k * f_tile, f_tile))
            return 0

        lax.fori_loop(0, hidden // f_tile, one, 0)

    def first_half(m, f):
        x = xc[2 * m:2 * m + 2, :, :, :HALF].reshape(m_rows, HALF)
        rows = slice(m * m_rows, (m + 1) * m_rows)
        acc[rows, pl.ds(f, f_tile)] = jnp.dot(
            x, wg[:HALF, pl.ds(f, f_tile)], preferred_element_type=F32
        )
        acc[rows, pl.ds(hidden + f, f_tile)] = jnp.dot(
            x, wu[:HALF, pl.ds(f, f_tile)], preferred_element_type=F32
        )

    def second_half(m, f):
        x = xc[2 * m:2 * m + 2, :, :, HALF:]
        x = x.reshape(m_rows, x.shape[-1])
        rows = slice(m * m_rows, (m + 1) * m_rows)
        gate = acc[rows, pl.ds(f, f_tile)] + jnp.dot(
            x, wg[HALF:, pl.ds(f, f_tile)], preferred_element_type=F32
        )
        up = acc[rows, pl.ds(hidden + f, f_tile)] + jnp.dot(
            x, wu[HALF:, pl.ds(f, f_tile)], preferred_element_type=F32
        )
        value = (gate / (1.0 + jnp.exp(-gate)) * up).astype(BF16)
        hid[2 * m:2 * m + 2, :, :, pl.ds(f, f_tile)] = value.reshape(2, SIDE, group, f_tile)

    for p in range(3):
        collect(p)
    for copy in load_w:
        copy.wait()
    up_tiles(first_half)
    for p in range(3, n):
        collect(p)
    up_tiles(second_half)

    def reorder_hidden(t):
        def reorder(i, _):
            src = hid.at[i] if t == 1 else hid.at[:, i]
            dst = hidp.at[t - 1, i] if t == 1 else hidp.at[t - 1, :, i]
            res = jnp.dot(
                swap[...], src[...].reshape(slab, hidden), preferred_element_type=F32
            )
            dst[...] = res.astype(BF16).reshape(SIDE, group, hidden)
            return 0

        lax.fori_loop(0, SIDE, reorder, 0)

    y_copies = {}

    def give_back(p):
        t, first, width = PIECES[p]
        a, b = PLANES[t]
        source = hid if t == 0 else hidp.at[t - 1]

        def down(i, _):
            res = jnp.dot(
                source[i].reshape(slab, hidden), wd[:, first:first + width],
                preferred_element_type=F32,
            )
            xs[p][i] = res.astype(BF16).reshape(SIDE, group, width)
            return 0

        lax.fori_loop(0, SIDE, down, 0)
        for o, (i, j) in enumerate(ORDER):
            copy = remote(
                xs[p].at[near[a][i], near[b][j]], yr[p].at[here[a], here[b]],
                y_send.at[p, o], y_recv.at[p, o], device(in_plane(t, i, j), core),
            )
            copy.start()
            y_copies[p, o] = copy
        yr[p][here[a], here[b]] = xs[p][here[a], here[b]]

    for p in range(n):
        t = PIECES[p][0]
        if p < 3 and t > 0:
            reorder_hidden(t)
        give_back(p)

    for copy in l_copies.values():
        copy.wait_send()
    for copy in m_copies.values():
        copy.wait_send()
    p_copies, z_copies = {}, {}
    half = SIDE * tokens

    def share(p):
        rows = slice(half * (p // 4), half * (p // 4 + 1))
        columns = slice(384 * (p % 4), 384 * (p % 4) + PIECES[p][2])
        return acc.at[rows, columns]

    def combine(p):
        t, first, width = PIECES[p]
        for o in range(len(ORDER)):
            y_copies[p, o].wait()

        def part(o):
            rows = pl.ds(pl.multiple_of(o * half, half), half)
            return jnp.dot(
                sel[t, rows, :], yr[p][...].reshape(total, width), preferred_element_type=F32
            )

        tokg[p][:, 0] = part(1 - core).astype(BF16).reshape(SIDE, tokens, width)
        copy = remote(
            tokg[p].at[:, 0], pr[p], p_send.at[p], p_recv.at[p], device((0, 0, 0), 1 - core)
        )
        copy.start()
        p_copies[p] = copy
        share(p)[...] = part(core)

    def reduce_cores(p):
        t, first, width = PIECES[p]
        p_copies[p].wait()
        both = share(p)[...] + pr[p][...].reshape(half, width).astype(F32)
        share(p)[...] = both
        tokg[p][:, 1] = both.astype(BF16).reshape(SIDE, tokens, width)
        for d in LINE:
            copy = remote(
                tokg[p].at[near[t][d], 1], zr[p].at[d - 1],
                z_send.at[p, d], z_recv.at[p, d], device(on_line(t, d), core),
            )
            copy.start()
            z_copies[p, d] = copy

    def finish(p):
        t, first, width = PIECES[p]
        result = share(p)[pl.ds(pl.multiple_of(here[t] * tokens, tokens), tokens), :]
        for d in LINE:
            z_copies[p, d].wait()
        for d in range(1, SIDE):
            result = result + zr[p][d - 1].astype(F32)
        out_ref[:, first:first + width] = result.astype(BF16)

    for p in range(n):
        combine(p)
        if p:
            reduce_cores(p - 1)
    reduce_cores(n - 1)
    for p in range(n):
        finish(p)


def body(tokens, expert_ids, gate_probs, w_gate, w_up, w_down):
    count, choices = expert_ids.shape
    width = tokens.shape[1]
    hidden = w_gate.shape[2]
    slots = 10
    group = 2 * SIDE * slots
    total = SIDE * SIDE * group
    n = len(PIECES)
    any_spec = pl.BlockSpec(memory_space=pl.ANY)
    dma = pltpu.SemaphoreType.DMA
    widths = [w for _, _, w in PIECES]
    scratch = (
        [pltpu.VMEM((SIDE, 2, count, w), BF16) for w in widths]
        + [pltpu.VMEM((SIDE, SIDE, group, w), BF16) for w in widths]
        + [pltpu.VMEM((SIDE, SIDE, group, w), BF16) for w in widths]
        + [pltpu.VMEM((SIDE, count, w), BF16) for w in widths]
        + [pltpu.VMEM((SIDE - 1, count, w), BF16) for w in widths]
        + [
            pltpu.VMEM((choices, count), jnp.int32),
            pltpu.VMEM((choices, count), F32),
            pltpu.VMEM((width, hidden), BF16),
            pltpu.VMEM((width, hidden), BF16),
            pltpu.VMEM((hidden, width), BF16),
            pltpu.VMEM((3, SIDE, 2, 2, 16, count), BF16),
            pltpu.VMEM((3, 2 * SIDE, 2, 16, count), BF16),
            pltpu.VMEM((16, count), F32),
            pltpu.VMEM((3, total, total), BF16),
            pltpu.VMEM((SIDE * group, SIDE * group), BF16),
            pltpu.VMEM((16, total), BF16),
            pltpu.VMEM((SIDE, SIDE, group, width), BF16),
            pltpu.VMEM((total, 2 * hidden), F32),
            pltpu.VMEM((SIDE, SIDE, group, hidden), BF16),
            pltpu.VMEM((2, SIDE, SIDE, group, hidden), BF16),
            dma((5 + n,)),
            dma((3, SIDE, 2)), dma((3, SIDE, 2)),
            dma((n, SIDE)), dma((n, SIDE)),
            dma((n, SIDE)), dma((n, SIDE)),
            dma((n, SIDE * SIDE - 1)), dma((n, SIDE * SIDE - 1)),
            dma((n, SIDE * SIDE - 1)), dma((n, SIDE * SIDE - 1)),
            dma((n,)), dma((n,)),
            dma((n, SIDE)), dma((n, SIDE)),
        ]
    )
    return pl.pallas_call(
        functools.partial(moe_kernel, slots),
        out_shape=jax.ShapeDtypeStruct((count, width), BF16),
        in_specs=[any_spec] * 6,
        out_specs=pl.BlockSpec(memory_space=pltpu.VMEM),
        scratch_shapes=scratch,
        compiler_params=pltpu.CompilerParams(
            collective_id=0, has_side_effects=True, vmem_limit_bytes=67043328
        ),
    )(expert_ids.T, gate_probs.T, tokens, w_gate, w_up, w_down)


def solution(mesh):
    in_specs = (
        P(("row", "col"), None),
        P(("row", "col"), None),
        P(("row", "col"), None),
        P(("row", "col"), None, None),
        P(("row", "col"), None, None),
        P(("row", "col"), None, None),
    )
    out_specs = P(("row", "col"), None)
    return jax.shard_map(body, mesh=mesh, in_specs=in_specs, out_specs=out_specs, check_vma=False)
```

time: 296 us -> 141 us (0.48)
  the two profiles are of different devices: /device:TPU:46 before, /device:TPU:1 now
where the time goes in v1:
time: 141 us
  Pallas kernels  139 us (99%)
  local copies, waits for them, and re-layouts  1.88 us (1%)
    pallas_call x1, Pallas kernels, body(): pl.pallas_call(functools.partial(moe_kernel, slots), out_shape=jax.ShapeD...  139 us

profile of v1, /device:TPU:1, one launch (start us, length us, event | category | flops | bytes accessed | tf_op | source)
XLA Modules:
  0.0 141.1 jit_solution(3322009128769256688)
XLA Ops:
  0.0 139.2 %shard_map.64 = bf16[128,2048]{1,0:T(8,128)(2,1)} custom-call(s32[8,128]{1,0:T(8,128)} %bitcast.2, f32[8,128]{1,0:T(8,128)} %bitcast.3, bf16[128,2048]{1,0:T(8,128)(2,1)} %tok_in.1, bf16[1,2048,768]{2,1,0:T(8,128)(2,1)} %wg_in.1, bf16[1,2048,768]{2,1,0:T(8,128)(2,1)} %wu_in.1, bf16[1,768,2048]{2,1,0:T(8,128)(2,1)} %wd_in.1), custom_call_target="tpu_custom_call" | custom-call | tf_op jit(solution)/shard_map/pallas_call | solution.py:494
  139.2 1.9 %copy.8 = bf16[128,2048]{1,0:T(8,128)(2,1)} copy(bf16[128,2048]{1,0:T(8,128)(2,1)} %shard_map.64) | data formatting | bytes 1048576

commit v2 on v1

--- a/solution.py
+++ b/solution.py
@@ -12,12 +12,16 @@
 F32 = jnp.float32
 SIDE = 4
 PIECES = (
-    (0, 0, 384), (1, 384, 384), (2, 768, 384),
-    (0, 1152, 384), (1, 1536, 256), (2, 1792, 256),
+    (0, 0, 128), (1, 128, 128), (2, 256, 128),
+    (0, 384, 384), (1, 768, 256), (2, 1024, 256),
+    (0, 1280, 256), (1, 1536, 256), (2, 1792, 256),
 )
-HALF = 1152
+TRIOS = ((0, 1, 2), (3, 4, 5), (6, 7, 8))
+RETURNS = (TRIOS[1], TRIOS[2], TRIOS[0])
+HALF = 1280
+SHARES = ((0, 896), (0, 1024), (0, 1152), (0, 0), (0, 384), (0, 640), (1, 0), (1, 256), (1, 512))
 PLANES = ((2, 1), (2, 0), (0, 1))
-ORDER = tuple((i, j) for i in range(SIDE) for j in range(SIDE) if i or j)
+PEERS = tuple((i, j) for i in range(SIDE) for j in range(SIDE) if i or j)
 LINE = (1, 3, 2)
 UNNAMED = -1024.0
 
@@ -34,7 +38,7 @@
     zr, scratch = scratch[:n], scratch[n:]
     (
         ids, probs, wg, wu, wd, kw_out, kw_in, kf, sel, swap, spread, xc, acc, hid, hidp,
-        load_sem, k_send, k_recv, l_send, l_recv, m_send, m_recv, x_send, x_recv,
+        load_sem, ready, k_send, k_recv, l_send, l_recv, m_send, m_recv, x_send, x_recv,
         y_send, y_recv, p_send, p_recv, z_send, z_recv,
     ) = scratch
     r = lax.axis_index("row")
@@ -85,22 +89,14 @@
         copy.start()
         load_tok.append(copy)
     barrier = pltpu.get_barrier_semaphore()
-    signals = 0
-    for dx in range(SIDE):
-        for dy in range(SIDE):
-            for dz in range(SIDE):
-                zeros = (dx == 0) + (dy == 0) + (dz == 0)
-                if zeros in (1, 2):
-                    pl.semaphore_signal(
-                        barrier, inc=1, device_id=device((dx, dy, dz), core), device_id_type=MESH
-                    )
-                    signals += 1
-                if zeros in (2, 3):
-                    pl.semaphore_signal(
-                        barrier, inc=1, device_id=device((dx, dy, dz), 1 - core),
-                        device_id_type=MESH,
-                    )
-                    signals += 1
+
+    def greet(semaphore, to):
+        pl.semaphore_signal(semaphore, inc=1, device_id=to, device_id_type=MESH)
+
+    greet(barrier, device((0, 0, 0), 1 - core))
+    for d in LINE:
+        for t in range(3):
+            greet(barrier, device(on_line(t, d), core))
 
     load_ids.wait()
     load_probs.wait()
@@ -142,21 +138,22 @@
                 kw_out[t, l, o, 1] = weight[rows]
         kw_in[t, 2 * here[t] + core] = kw_out[t, here[t], core]
 
-    pl.semaphore_wait(barrier, signals)
+    pl.semaphore_wait(barrier, 1 + 3 * len(LINE))
+    greet(ready.at[0], device((0, 0, 0), 1 - core))
+    for d in LINE:
+        for t in range(3):
+            greet(ready.at[1], device(on_line(t, d), core))
 
     k_copies = []
-    for t in range(3):
-        for d in range(SIDE):
-            for o in range(2):
-                if d == 0 and o == 0:
-                    continue
-                to_core = core if o == 0 else 1 - core
-                copy = remote(
-                    kw_out.at[t, near[t][d], to_core], kw_in.at[t, 2 * here[t] + core],
-                    k_send.at[t, d, o], k_recv.at[t, d, o], device(on_line(t, d), to_core),
-                )
-                copy.start()
-                k_copies.append(copy)
+
+    def send_keys(t, d, o):
+        to_core = core if o == 0 else 1 - core
+        copy = remote(
+            kw_out.at[t, near[t][d], to_core], kw_in.at[t, 2 * here[t] + core],
+            k_send.at[t, d, o], k_recv.at[t, d, o], device(on_line(t, d), to_core),
+        )
+        copy.start()
+        k_copies.append(copy)
 
     l_copies = {}
     m_copies = {}
@@ -170,16 +167,32 @@
         copy.start()
         m_copies[p, d] = copy
 
-    for p, (t, first, width) in enumerate(PIECES):
-        load_tok[p].wait()
+    def send_tokens(trio):
+        for p in trio:
+            load_tok[p].wait()
         for d in LINE:
-            block = tokg[p].at[here[t], core]
-            copy = remote(
-                block, block, l_send.at[p, d], l_recv.at[p, d], device(on_line(t, d), core)
-            )
-            copy.start()
-            l_copies[p, d] = copy
-        to_mate(p, 0)
+            for p in trio:
+                t = PIECES[p][0]
+                block = tokg[p].at[here[t], core]
+                copy = remote(
+                    block, block, l_send.at[p, d], l_recv.at[p, d], device(on_line(t, d), core)
+                )
+                copy.start()
+                l_copies[p, d] = copy
+        for p in trio:
+            to_mate(p, 0)
+
+    send_tokens(TRIOS[0])
+    for t in range(3):
+        for d in LINE:
+            send_keys(t, d, 0)
+        send_keys(t, 0, 1)
+    pl.semaphore_wait(ready.at[0], 1)
+    for t in range(3):
+        for d in LINE:
+            send_keys(t, d, 1)
+    for trio in TRIOS[1:]:
+        send_tokens(trio)
     for copy in load_w:
         copy.start()
 
@@ -214,6 +227,44 @@
 
         lax.fori_loop(0, 2 * SIDE, choose, 0)
 
+    def exchange(trio, product, landing, send, recv):
+        copies = {}
+
+        def peer(p, i, j, v):
+            a, b = PLANES[PIECES[p][0]]
+            at = list(here)
+            at[a], at[b] = v, near[b][j]
+            return remote(
+                xs[p].at[v, near[b][j]], landing(p, here[a], here[b]),
+                send.at[p, i, j], recv.at[p, i, j],
+                (SIDE * (at[2] // 2) + at[0], 8 * (at[2] % 2) + 2 * at[1] + core),
+            )
+
+        def slab_of(i, _):
+            where = []
+            for p in trio:
+                v = (here[PLANES[PIECES[p][0]][0]] + sign * i + SIDE) % SIDE
+                xs[p][v] = product(p, v).astype(BF16).reshape(SIDE, group, PIECES[p][2])
+                where.append(v)
+
+            @pl.when(i > 0)
+            def _():
+                for p, v in zip(trio, where):
+                    peer(p, i, 0, v).start()
+
+            for j in range(1, SIDE):
+                for p, v in zip(trio, where):
+                    peer(p, i, j, v).start()
+            return 0
+
+        lax.fori_loop(0, SIDE, slab_of, 0)
+        for p in trio:
+            a, b = PLANES[PIECES[p][0]]
+            landing(p, here[a], here[b])[...] = xs[p][here[a], here[b]]
+            for i, j in PEERS:
+                copies[p, i, j] = peer(p, i, j, near[a][i])
+        return copies
+
     sources = 2 * SIDE * tokens
     x_copies = {}
 
@@ -222,40 +273,29 @@
             l_copies[p, d].wait_recv()
             to_mate(p, d)
 
-    def dispatch(p):
+    def select(p, v):
         t, first, width = PIECES[p]
-        a, b = PLANES[t]
-        for d in range(SIDE):
-            m_copies[p, d].wait_recv()
-
-        def select(i, _):
-            rows = pl.ds(pl.multiple_of(i * slab, slab), slab)
-            res = jnp.dot(
-                sel[t, rows, :sources], tokg[p][...].reshape(sources, width),
-                preferred_element_type=F32,
-            )
-            xs[p][i] = res.astype(BF16).reshape(SIDE, group, width)
-            return 0
-
-        lax.fori_loop(0, SIDE, select, 0)
-        columns = pl.ds(first, width)
-        for o, (i, j) in enumerate(ORDER):
-            copy = remote(
-                xs[p].at[near[a][i], near[b][j]], xc.at[here[a], here[b], :, columns],
-                x_send.at[p, o], x_recv.at[p, o], device(in_plane(t, i, j), core),
-            )
-            copy.start()
-            x_copies[p, o] = copy
-        xc[here[a], here[b], :, columns] = xs[p][here[a], here[b]]
-
-    for p in range(3):
+        rows = pl.ds(pl.multiple_of(v * slab, slab), slab)
+        return jnp.dot(
+            sel[t, rows, :sources], tokg[p][...].reshape(sources, width),
+            preferred_element_type=F32,
+        )
+
+    def arrival(p, u, v):
+        return xc.at[u, v, :, pl.ds(PIECES[p][1], PIECES[p][2])]
+
+    for p in TRIOS[0]:
         forward(p)
-    for p in range(3):
-        dispatch(p)
-    for p in range(3, n):
-        forward(p)
-    for p in range(3, n):
-        dispatch(p)
+    for trio in TRIOS:
+        for p in trio:
+            for d in range(SIDE):
+                m_copies[p, d].wait_recv()
+        if trio == TRIOS[0]:
+            pl.semaphore_wait(ready.at[1], 3 * len(LINE))
+        x_copies.update(exchange(trio, select, arrival, x_send, x_recv))
+        if trio != TRIOS[-1]:
+            for p in TRIOS[TRIOS.index(trio) + 1]:
+                forward(p)
 
     lane = lax.broadcasted_iota(jnp.int32, (1, total), 1)
     slot_at = lane
@@ -283,8 +323,8 @@
 
     def collect(p):
         t, first, width = PIECES[p]
-        for o in range(len(ORDER)):
-            x_copies[p, o].wait()
+        for i, j in PEERS:
+            x_copies[p, i, j].wait()
         if t == 0:
             return
         columns = pl.ds(first, width)
@@ -333,12 +373,12 @@
         value = (gate / (1.0 + jnp.exp(-gate)) * up).astype(BF16)
         hid[2 * m:2 * m + 2, :, :, pl.ds(f, f_tile)] = value.reshape(2, SIDE, group, f_tile)
 
-    for p in range(3):
+    for p in TRIOS[0] + TRIOS[1]:
         collect(p)
     for copy in load_w:
         copy.wait()
     up_tiles(first_half)
-    for p in range(3, n):
+    for p in TRIOS[2]:
         collect(p)
     up_tiles(second_half)
 
@@ -356,34 +396,18 @@
 
     y_copies = {}
 
-    def give_back(p):
+    def down(p, v):
         t, first, width = PIECES[p]
-        a, b = PLANES[t]
         source = hid if t == 0 else hidp.at[t - 1]
-
-        def down(i, _):
-            res = jnp.dot(
-                source[i].reshape(slab, hidden), wd[:, first:first + width],
-                preferred_element_type=F32,
-            )
-            xs[p][i] = res.astype(BF16).reshape(SIDE, group, width)
-            return 0
-
-        lax.fori_loop(0, SIDE, down, 0)
-        for o, (i, j) in enumerate(ORDER):
-            copy = remote(
-                xs[p].at[near[a][i], near[b][j]], yr[p].at[here[a], here[b]],
-                y_send.at[p, o], y_recv.at[p, o], device(in_plane(t, i, j), core),
-            )
-            copy.start()
-            y_copies[p, o] = copy
-        yr[p][here[a], here[b]] = xs[p][here[a], here[b]]
-
-    for p in range(n):
-        t = PIECES[p][0]
-        if p < 3 and t > 0:
-            reorder_hidden(t)
-        give_back(p)
+        return jnp.dot(
+            source[v].reshape(slab, hidden), wd[:, first:first + width],
+            preferred_element_type=F32,
+        )
+
+    for t in (1, 2):
+        reorder_hidden(t)
+    for trio in RETURNS:
+        y_copies.update(exchange(trio, down, lambda p, u, v: yr[p].at[u, v], y_send, y_recv))
 
     for copy in l_copies.values():
         copy.wait_send()
@@ -393,14 +417,13 @@
     half = SIDE * tokens
 
     def share(p):
-        rows = slice(half * (p // 4), half * (p // 4 + 1))
-        columns = slice(384 * (p % 4), 384 * (p % 4) + PIECES[p][2])
-        return acc.at[rows, columns]
+        band, first = SHARES[p]
+        return acc.at[half * band:half * (band + 1), first:first + PIECES[p][2]]
 
     def combine(p):
         t, first, width = PIECES[p]
-        for o in range(len(ORDER)):
-            y_copies[p, o].wait()
+        for i, j in PEERS:
+            y_copies[p, i, j].wait()
 
         def part(o):
             rows = pl.ds(pl.multiple_of(o * half, half), half)
@@ -439,12 +462,15 @@
             result = result + zr[p][d - 1].astype(F32)
         out_ref[:, first:first + width] = result.astype(BF16)
 
-    for p in range(n):
-        combine(p)
-        if p:
-            reduce_cores(p - 1)
-    reduce_cores(n - 1)
-    for p in range(n):
+    for trio in RETURNS:
+        for p in trio:
+            combine(p)
+        if trio != RETURNS[0]:
+            for p in RETURNS[RETURNS.index(trio) - 1]:
+                finish(p)
+        for p in trio:
+            reduce_cores(p)
+    for p in RETURNS[-1]:
         finish(p)
 
 
@@ -482,11 +508,12 @@
             pltpu.VMEM((SIDE, SIDE, group, hidden), BF16),
             pltpu.VMEM((2, SIDE, SIDE, group, hidden), BF16),
             dma((5 + n,)),
+            pltpu.SemaphoreType.REGULAR((2,)),
             dma((3, SIDE, 2)), dma((3, SIDE, 2)),
             dma((n, SIDE)), dma((n, SIDE)),
             dma((n, SIDE)), dma((n, SIDE)),
-            dma((n, SIDE * SIDE - 1)), dma((n, SIDE * SIDE - 1)),
-            dma((n, SIDE * SIDE - 1)), dma((n, SIDE * SIDE - 1)),
+            dma((n, SIDE, SIDE)), dma((n, SIDE, SIDE)),
+            dma((n, SIDE, SIDE)), dma((n, SIDE, SIDE)),
             dma((n,)), dma((n,)),
             dma((n, SIDE)), dma((n, SIDE)),
         ]

time: 141 us -> 136 us (0.965)
  Pallas kernels: 139 us -> 134 us
    pallas_call x1, Pallas kernels: 139 us -> 134 us  [body(): pl.pallas_call(functools.partial(moe_kernel, slots), out_shape=jax.ShapeD...]
where the time goes in v2:
time: 136 us
  Pallas kernels  134 us (99%)
  local copies, waits for them, and re-layouts  1.88 us (1%)
    pallas_call x1, Pallas kernels, body(): pl.pallas_call(functools.partial(moe_kernel, slots), out_shape=jax.ShapeD...  134 us

profile of v2, /device:TPU:1, one launch (start us, length us, event | category | flops | bytes accessed | tf_op | source)
XLA Modules:
  0.0 135.7 jit_solution(3067022231599150975)
XLA Ops:
  0.0 133.8 %shard_map.64 = bf16[128,2048]{1,0:T(8,128)(2,1)} custom-call(s32[8,128]{1,0:T(8,128)} %bitcast.2, f32[8,128]{1,0:T(8,128)} %bitcast.3, bf16[128,2048]{1,0:T(8,128)(2,1)} %tok_in.1, bf16[1,2048,768]{2,1,0:T(8,128)(2,1)} %wg_in.1, bf16[1,2048,768]{2,1,0:T(8,128)(2,1)} %wu_in.1, bf16[1,768,2048]{2,1,0:T(8,128)(2,1)} %wd_in.1), custom_call_target="tpu_custom_call" | custom-call | tf_op jit(solution)/shard_map/pallas_call | solution.py:521
  133.8 1.9 %copy.8 = bf16[128,2048]{1,0:T(8,128)(2,1)} copy(bf16[128,2048]{1,0:T(8,128)(2,1)} %shard_map.64) | data formatting | bytes 1048576

commit v3 on v2

--- a/solution.py
+++ b/solution.py
@@ -144,7 +144,7 @@
         for t in range(3):
             greet(ready.at[1], device(on_line(t, d), core))
 
-    k_copies = []
+    k_copies = {}
 
     def send_keys(t, d, o):
         to_core = core if o == 0 else 1 - core
@@ -153,7 +153,7 @@
             k_send.at[t, d, o], k_recv.at[t, d, o], device(on_line(t, d), to_core),
         )
         copy.start()
-        k_copies.append(copy)
+        k_copies[t, d, o] = copy
 
     l_copies = {}
     m_copies = {}
@@ -182,11 +182,11 @@
         for p in trio:
             to_mate(p, 0)
 
-    send_tokens(TRIOS[0])
     for t in range(3):
         for d in LINE:
             send_keys(t, d, 0)
         send_keys(t, 0, 1)
+    send_tokens(TRIOS[0])
     pl.semaphore_wait(ready.at[0], 1)
     for t in range(3):
         for d in LINE:
@@ -212,8 +212,11 @@
     owner = group * lax.broadcasted_iota(jnp.int32, (16, total), 0)
     spread[...] = ((lane >= owner) & (lane < owner + group)).astype(F32).astype(BF16)
 
-    for copy in k_copies:
-        copy.wait()
+    def forward(p):
+        for d in LINE:
+            l_copies[p, d].wait_recv()
+            to_mate(p, d)
+
     slot_of = lax.broadcasted_iota(jnp.int32, (group, tokens), 0).astype(F32)
     for t in range(3):
         def choose(s, _):
@@ -225,9 +228,15 @@
                 ).astype(F32).astype(BF16)
             return 0
 
+        for (kind, d, o), copy in k_copies.items():
+            if kind == t:
+                copy.wait()
         lax.fori_loop(0, 2 * SIDE, choose, 0)
-
-    def exchange(trio, product, landing, send, recv):
+        if t == 0:
+            for p in TRIOS[0]:
+                forward(p)
+
+    def exchange(trio, product, landing, send, recv, prepare=None):
         copies = {}
 
         def peer(p, i, j, v):
@@ -242,6 +251,8 @@
 
         def slab_of(i, _):
             where = []
+            if prepare is not None:
+                prepare((here[PLANES[PIECES[trio[0]][0]][0]] + sign * i + SIDE) % SIDE)
             for p in trio:
                 v = (here[PLANES[PIECES[p][0]][0]] + sign * i + SIDE) % SIDE
                 xs[p][v] = product(p, v).astype(BF16).reshape(SIDE, group, PIECES[p][2])
@@ -267,11 +278,6 @@
 
     sources = 2 * SIDE * tokens
     x_copies = {}
-
-    def forward(p):
-        for d in LINE:
-            l_copies[p, d].wait_recv()
-            to_mate(p, d)
 
     def select(p, v):
         t, first, width = PIECES[p]
@@ -284,8 +290,6 @@
     def arrival(p, u, v):
         return xc.at[u, v, :, pl.ds(PIECES[p][1], PIECES[p][2])]
 
-    for p in TRIOS[0]:
-        forward(p)
     for trio in TRIOS:
         for p in trio:
             for d in range(SIDE):
@@ -321,78 +325,79 @@
 
         lax.fori_loop(0, SIDE, weigh_all, 0)
 
-    def collect(p):
-        t, first, width = PIECES[p]
+    def arrive(p):
         for i, j in PEERS:
             x_copies[p, i, j].wait()
-        if t == 0:
-            return
+
+    def reorder(p, i):
+        t, first, width = PIECES[p]
+        block = xc.at[i] if t == 1 else xc.at[:, i]
         columns = pl.ds(first, width)
-
-        def reorder(i, _):
-            block = xc.at[i] if t == 1 else xc.at[:, i]
-            res = jnp.dot(
-                swap[...], block[:, :, columns].reshape(slab, width), preferred_element_type=F32
-            )
-            block[:, :, columns] = res.astype(BF16).reshape(SIDE, group, width)
+        res = jnp.dot(
+            swap[...], block[:, :, columns].reshape(slab, width), preferred_element_type=F32
+        )
+        block[:, :, columns] = res.astype(BF16).reshape(SIDE, group, width)
+
+    def reorder_all(p):
+        def one(i, _):
+            reorder(p, i)
             return 0
 
-        lax.fori_loop(0, SIDE, reorder, 0)
-
+        lax.fori_loop(0, SIDE, one, 0)
+
+    f_tile = 256
     m_rows = 2 * slab
-    f_tile = 256
-
-    def up_tiles(step):
+
+    def first_half(k, _):
+        f = pl.multiple_of(k * f_tile, f_tile)
+        for m in range(2):
+            x = xc[2 * m:2 * m + 2, :, :, :HALF].reshape(m_rows, HALF)
+            rows = slice(m * m_rows, (m + 1) * m_rows)
+            acc[rows, pl.ds(f, f_tile)] = jnp.dot(
+                x, wg[:HALF, pl.ds(f, f_tile)], preferred_element_type=F32
+            )
+            acc[rows, pl.ds(hidden + f, f_tile)] = jnp.dot(
+                x, wu[:HALF, pl.ds(f, f_tile)], preferred_element_type=F32
+            )
+        return 0
+
+    def reorder_hidden(t, i):
+        src = hid.at[i] if t == 1 else hid.at[:, i]
+        dst = hidp.at[t - 1, i] if t == 1 else hidp.at[t - 1, :, i]
+        res = jnp.dot(swap[...], src[...].reshape(slab, hidden), preferred_element_type=F32)
+        dst[...] = res.astype(BF16).reshape(SIDE, group, hidden)
+
+    def second_half(v):
+        reorder(TRIOS[2][1], v)
+        rows = pl.ds(pl.multiple_of(v * slab, slab), slab)
+
         def one(k, _):
-            for m in range(2):
-                step(m, pl.multiple_of(k * f_tile, f_tile))
+            f = pl.multiple_of(k * f_tile, f_tile)
+            x = xc[v, :, :, HALF:]
+            x = x.reshape(slab, x.shape[-1])
+            gate = acc[rows, pl.ds(f, f_tile)] + jnp.dot(
+                x, wg[HALF:, pl.ds(f, f_tile)], preferred_element_type=F32
+            )
+            up = acc[rows, pl.ds(hidden + f, f_tile)] + jnp.dot(
+                x, wu[HALF:, pl.ds(f, f_tile)], preferred_element_type=F32
+            )
+            value = (gate / (1.0 + jnp.exp(-gate)) * up).astype(BF16)
+            hid[v, :, :, pl.ds(f, f_tile)] = value.reshape(SIDE, group, f_tile)
             return 0
 
         lax.fori_loop(0, hidden // f_tile, one, 0)
-
-    def first_half(m, f):
-        x = xc[2 * m:2 * m + 2, :, :, :HALF].reshape(m_rows, HALF)
-        rows = slice(m * m_rows, (m + 1) * m_rows)
-        acc[rows, pl.ds(f, f_tile)] = jnp.dot(
-            x, wg[:HALF, pl.ds(f, f_tile)], preferred_element_type=F32
-        )
-        acc[rows, pl.ds(hidden + f, f_tile)] = jnp.dot(
-            x, wu[:HALF, pl.ds(f, f_tile)], preferred_element_type=F32
-        )
-
-    def second_half(m, f):
-        x = xc[2 * m:2 * m + 2, :, :, HALF:]
-        x = x.reshape(m_rows, x.shape[-1])
-        rows = slice(m * m_rows, (m + 1) * m_rows)
-        gate = acc[rows, pl.ds(f, f_tile)] + jnp.dot(
-            x, wg[HALF:, pl.ds(f, f_tile)], preferred_element_type=F32
-        )
-        up = acc[rows, pl.ds(hidden + f, f_tile)] + jnp.dot(
-            x, wu[HALF:, pl.ds(f, f_tile)], preferred_element_type=F32
-        )
-        value = (gate / (1.0 + jnp.exp(-gate)) * up).astype(BF16)
-        hid[2 * m:2 * m + 2, :, :, pl.ds(f, f_tile)] = value.reshape(2, SIDE, group, f_tile)
+        reorder_hidden(1, v)
 
     for p in TRIOS[0] + TRIOS[1]:
-        collect(p)
+        arrive(p)
+        if PIECES[p][0] > 0:
+            reorder_all(p)
     for copy in load_w:
         copy.wait()
-    up_tiles(first_half)
+    lax.fori_loop(0, hidden // f_tile, first_half, 0)
     for p in TRIOS[2]:
-        collect(p)
-    up_tiles(second_half)
-
-    def reorder_hidden(t):
-        def reorder(i, _):
-            src = hid.at[i] if t == 1 else hid.at[:, i]
-            dst = hidp.at[t - 1, i] if t == 1 else hidp.at[t - 1, :, i]
-            res = jnp.dot(
-                swap[...], src[...].reshape(slab, hidden), preferred_element_type=F32
-            )
-            dst[...] = res.astype(BF16).reshape(SIDE, group, hidden)
-            return 0
-
-        lax.fori_loop(0, SIDE, reorder, 0)
+        arrive(p)
+    reorder_all(TRIOS[2][2])
 
     y_copies = {}
 
@@ -404,10 +409,20 @@
             preferred_element_type=F32,
         )
 
-    for t in (1, 2):
-        reorder_hidden(t)
-    for trio in RETURNS:
-        y_copies.update(exchange(trio, down, lambda p, u, v: yr[p].at[u, v], y_send, y_recv))
+    def reorder_last(i, _):
+        reorder_hidden(2, i)
+        return 0
+
+    def give_back(trio, prepare=None):
+        y_copies.update(
+            exchange(trio, down, lambda p, u, v: yr[p].at[u, v], y_send, y_recv, prepare)
+        )
+
+    give_back(RETURNS[0][:2], second_half)
+    lax.fori_loop(0, SIDE, reorder_last, 0)
+    give_back(RETURNS[0][2:])
+    for trio in RETURNS[1:]:
+        give_back(trio)
 
     for copy in l_copies.values():
         copy.wait_send()
@@ -420,24 +435,25 @@
         band, first = SHARES[p]
         return acc.at[half * band:half * (band + 1), first:first + PIECES[p][2]]
 
-    def combine(p):
-        t, first, width = PIECES[p]
-        for i, j in PEERS:
-            y_copies[p, i, j].wait()
-
-        def part(o):
-            rows = pl.ds(pl.multiple_of(o * half, half), half)
-            return jnp.dot(
-                sel[t, rows, :], yr[p][...].reshape(total, width), preferred_element_type=F32
-            )
-
-        tokg[p][:, 0] = part(1 - core).astype(BF16).reshape(SIDE, tokens, width)
-        copy = remote(
-            tokg[p].at[:, 0], pr[p], p_send.at[p], p_recv.at[p], device((0, 0, 0), 1 - core)
-        )
-        copy.start()
-        p_copies[p] = copy
-        share(p)[...] = part(core)
+    def part(p, o):
+        rows = pl.ds(pl.multiple_of(o * half, half), half)
+        return jnp.dot(
+            sel[PIECES[p][0], rows, :], yr[p][...].reshape(total, PIECES[p][2]),
+            preferred_element_type=F32,
+        )
+
+    def combine(trio):
+        for p in trio:
+            for i, j in PEERS:
+                y_copies[p, i, j].wait()
+            tokg[p][:, 0] = part(p, 1 - core).astype(BF16).reshape(SIDE, tokens, PIECES[p][2])
+            copy = remote(
+                tokg[p].at[:, 0], pr[p], p_send.at[p], p_recv.at[p], device((0, 0, 0), 1 - core)
+            )
+            copy.start()
+            p_copies[p] = copy
+        for p in trio:
+            share(p)[...] = part(p, core)
 
     def reduce_cores(p):
         t, first, width = PIECES[p]
@@ -462,16 +478,16 @@
             result = result + zr[p][d - 1].astype(F32)
         out_ref[:, first:first + width] = result.astype(BF16)
 
-    for trio in RETURNS:
-        for p in trio:
-            combine(p)
-        if trio != RETURNS[0]:
-            for p in RETURNS[RETURNS.index(trio) - 1]:
+    for k, trio in enumerate(RETURNS):
+        combine(trio)
+        for p in trio:
+            reduce_cores(p)
+        if k == 1:
+            for p in RETURNS[0]:
                 finish(p)
-        for p in trio:
-            reduce_cores(p)
-    for p in RETURNS[-1]:
-        finish(p)
+    for trio in RETURNS[1:]:
+        for p in trio:
+            finish(p)
 
 
 def body(tokens, expert_ids, gate_probs, w_gate, w_up, w_down):

time: 136 us -> 131 us (0.963)
  Pallas kernels: 134 us -> 129 us
    pallas_call x1, Pallas kernels: 134 us -> 129 us  [body(): pl.pallas_call(functools.partial(moe_kernel, slots), out_shape=jax.ShapeD...]
where the time goes in v3:
time: 131 us
  Pallas kernels  129 us (98%)
  local copies, waits for them, and re-layouts  1.88 us (1%)
    pallas_call x1, Pallas kernels, body(): pl.pallas_call(functools.partial(moe_kernel, slots), out_shape=jax.ShapeD...  129 us

profile of v3, /device:TPU:1, one launch (start us, length us, event | category | flops | bytes accessed | tf_op | source)
XLA Modules:
  0.0 131.1 jit_solution(168938059115391518)
XLA Ops:
  0.0 129.2 %shard_map.64 = bf16[128,2048]{1,0:T(8,128)(2,1)} custom-call(s32[8,128]{1,0:T(8,128)} %bitcast.2, f32[8,128]{1,0:T(8,128)} %bitcast.3, bf16[128,2048]{1,0:T(8,128)(2,1)} %tok_in.1, bf16[1,2048,768]{2,1,0:T(8,128)(2,1)} %wg_in.1, bf16[1,2048,768]{2,1,0:T(8,128)(2,1)} %wu_in.1, bf16[1,768,2048]{2,1,0:T(8,128)(2,1)} %wd_in.1), custom_call_target="tpu_custom_call" | custom-call | tf_op jit(solution)/shard_map/pallas_call | solution.py:537
  129.2 1.9 %copy.8 = bf16[128,2048]{1,0:T(8,128)(2,1)} copy(bf16[128,2048]{1,0:T(8,128)(2,1)} %shard_map.64) | data formatting | bytes 1048576

commit v4 on v3

--- a/solution.py
+++ b/solution.py
@@ -22,7 +22,7 @@
 SHARES = ((0, 896), (0, 1024), (0, 1152), (0, 0), (0, 384), (0, 640), (1, 0), (1, 256), (1, 512))
 PLANES = ((2, 1), (2, 0), (0, 1))
 PEERS = tuple((i, j) for i in range(SIDE) for j in range(SIDE) if i or j)
-LINE = (1, 3, 2)
+LINE = (2, 1, 3)
 UNNAMED = -1024.0
 
 
@@ -459,7 +459,6 @@
         t, first, width = PIECES[p]
         p_copies[p].wait()
         both = share(p)[...] + pr[p][...].reshape(half, width).astype(F32)
-        share(p)[...] = both
         tokg[p][:, 1] = both.astype(BF16).reshape(SIDE, tokens, width)
         for d in LINE:
             copy = remote(
@@ -472,6 +471,7 @@
     def finish(p):
         t, first, width = PIECES[p]
         result = share(p)[pl.ds(pl.multiple_of(here[t] * tokens, tokens), tokens), :]
+        result = result + pr[p][here[t]].astype(F32)
         for d in LINE:
             z_copies[p, d].wait()
         for d in range(1, SIDE):

time: 131 us -> 131 us (level)
  no operation moved by 1% of the time
where the time goes in v4:
time: 131 us; the launch traced here: 130 us
  Pallas kernels  129 us (98%)
  local copies, waits for them, and re-layouts  1.88 us (1%)
    pallas_call x1, Pallas kernels, body(): pl.pallas_call(functools.partial(moe_kernel, slots), out_shape=jax.ShapeD...  129 us

profile of v4, /device:TPU:1, one launch (start us, length us, event | category | flops | bytes accessed | tf_op | source)
XLA Modules:
  0.0 130.4 jit_solution(6782452548807982755)
XLA Ops:
  0.0 128.6 %shard_map.64 = bf16[128,2048]{1,0:T(8,128)(2,1)} custom-call(s32[8,128]{1,0:T(8,128)} %bitcast.2, f32[8,128]{1,0:T(8,128)} %bitcast.3, bf16[128,2048]{1,0:T(8,128)(2,1)} %tok_in.1, bf16[1,2048,768]{2,1,0:T(8,128)(2,1)} %wg_in.1, bf16[1,2048,768]{2,1,0:T(8,128)(2,1)} %wu_in.1, bf16[1,768,2048]{2,1,0:T(8,128)(2,1)} %wd_in.1), custom_call_target="tpu_custom_call" | custom-call | tf_op jit(solution)/shard_map/pallas_call | solution.py:537
  128.6 1.9 %copy.8 = bf16[128,2048]{1,0:T(8,128)(2,1)} copy(bf16[128,2048]{1,0:T(8,128)(2,1)} %shard_map.64) | data formatting | bytes 1048576

commit v5 on v4

--- a/solution.py
+++ b/solution.py
@@ -395,9 +395,10 @@
     for copy in load_w:
         copy.wait()
     lax.fori_loop(0, hidden // f_tile, first_half, 0)
-    for p in TRIOS[2]:
+    arrive(TRIOS[2][2])
+    reorder_all(TRIOS[2][2])
+    for p in TRIOS[2][:2]:
         arrive(p)
-    reorder_all(TRIOS[2][2])
 
     y_copies = {}
 

time: 131 us -> 130 us (level)
  no operation moved by 1% of the time
where the time goes in v5:
time: 130 us
  Pallas kernels  128 us (98%)
  local copies, waits for them, and re-layouts  1.88 us (1%)
    pallas_call x1, Pallas kernels, body(): pl.pallas_call(functools.partial(moe_kernel, slots), out_shape=jax.ShapeD...  128 us

profile of v5, /device:TPU:1, one launch (start us, length us, event | category | flops | bytes accessed | tf_op | source)
XLA Modules:
  0.0 129.6 jit_solution(16244332125412788670)
XLA Ops:
  0.0 127.7 %shard_map.64 = bf16[128,2048]{1,0:T(8,128)(2,1)} custom-call(s32[8,128]{1,0:T(8,128)} %bitcast.2, f32[8,128]{1,0:T(8,128)} %bitcast.3, bf16[128,2048]{1,0:T(8,128)(2,1)} %tok_in.1, bf16[1,2048,768]{2,1,0:T(8,128)(2,1)} %wg_in.1, bf16[1,2048,768]{2,1,0:T(8,128)(2,1)} %wu_in.1, bf16[1,768,2048]{2,1,0:T(8,128)(2,1)} %wd_in.1), custom_call_target="tpu_custom_call" | custom-call | tf_op jit(solution)/shard_map/pallas_call | solution.py:538
  127.7 1.9 %copy.8 = bf16[128,2048]{1,0:T(8,128)(2,1)} copy(bf16[128,2048]{1,0:T(8,128)(2,1)} %shard_map.64) | data formatting | bytes 1048576
